TPU v7x, 32 devices: a whole 2x2x4 slice. The times are simulated.
32 devices in a mesh: grp: 16 (over z, x, core), fsdp: 2 (over y).
Axes of the slice: x: 2, y: 2, z: 4, core: 2. Of those that a mesh axis runs over, the one named last changes fastest.
Arguments:
- normalized_inputs: bfloat16 [4096, 2048], P(('grp', 'fsdp')), may hold values from -6 to 6
- output_sensitivity: bfloat16 [4096, 512], P(('grp', 'fsdp')), may hold values from -6 to 6
- projection_weights: bfloat16 [2048, 512], P('fsdp'), may hold values from -0.25 to 0.25
- completion_mask: int32 [16], replicated, may hold values 0 or 1
- replica_partition_list: int32 [16], replicated, may hold values from 0 to 3, as said below
Outputs:
- input_grad: bfloat16 [4096, 2048], P(('grp', 'fsdp'))
- weight_grad: float32 [2048, 512], P(('grp', 'fsdp'))
Inputs may be any that keep to these rules, and one draw needn't show every extreme that they name: `replica_partition_list`: each of the 4 block numbers is named by exactly 4 groups.
All inputs are finite; a program needn't handle non-finite values.
Results may differ from a plain program's by a relative error of at most 0.001.
Values may be sent and summed in bfloat16 or wider, within the bound.
A program may use at most 64 MiB of HBM per device.

v0:
```python
import functools

import jax
import jax.numpy as jnp
from jax import lax
from jax.experimental import pallas as pl
from jax.experimental.pallas import tpu as pltpu
from jax.sharding import PartitionSpec as P

MESH = pl.DeviceIdType.MESH
CORES = 2
WIDE = 2
STEPS = 32766.0
TINY = 1e-33


def collective_shards(
    normalized_inputs,
    output_sensitivity,
    projection_weights,
    completion_mask,
    replica_partition_list,
):
    replica_index = lax.axis_index("grp")
    selected_replica = lax.iota(jnp.int32, completion_mask.shape[0]) == replica_index
    assigned_piece = jnp.sum(jnp.where(selected_replica, replica_partition_list, 0))
    finished_indicator = jnp.sum(jnp.where(selected_replica, completion_mask, 0))
    finisher_tally = jnp.sum(
        jnp.where(replica_partition_list == assigned_piece, completion_mask, 0)
    )
    living_float = finished_indicator.astype(jnp.float32)
    decode_sum = living_float / (finisher_tally.astype(jnp.float32) + 1.0 - living_float)
    tokens_here = normalized_inputs.shape[0]
    model_width = normalized_inputs.shape[1]
    inner_size = lax.axis_size("fsdp")
    outer_size = lax.axis_size("grp")
    input_grad = lax.dot_general(
        output_sensitivity,
        lax.all_gather(projection_weights, "fsdp", axis=0, tiled=True),
        (((1,), (1,)), ((), ())),
        preferred_element_type=jnp.float32,
    ).astype(jnp.bfloat16)
    owner_rows = model_width // (outer_size * inner_size)
    reordered = normalized_inputs.reshape(tokens_here, outer_size, inner_size, owner_rows)
    reordered = reordered.transpose(0, 2, 1, 3).reshape(tokens_here, model_width)
    column_block = lax.all_to_all(reordered, "fsdp", split_axis=1, concat_axis=0, tiled=True)
    group_block = lax.dot_general(
        column_block,
        lax.all_gather(output_sensitivity, "fsdp", axis=0, tiled=True),
        (((0,), (0,)), ((), ())),
        preferred_element_type=jnp.float32,
    )
    weight_grad = lax.psum_scatter(decode_sum * group_block, "grp", scatter_dimension=0, tiled=True)
    return (input_grad, weight_grad)


def encode(value):
    top = jnp.maximum(jnp.max(jnp.abs(value), axis=0, keepdims=True), TINY)
    coded = jnp.round(value * (STEPS / top)).astype(jnp.int32).astype(jnp.int16)
    return coded, top * (1.0 / STEPS)


def decoded(coded, step):
    return coded.astype(jnp.int32).astype(jnp.float32) * step


def kernel(
    deep,
    mask_ref, list_ref, x_hbm, s_hbm, w_hbm,
    ig_ref, wg_ref,
    x_v, s_v, w_v, tx, rx, own_part, px_send, px_scale, px_recv, px_rscale,
    q, q_send, q_scale, zr, zr_scale, ig_send,
    load_sem, s_send_sem, s_recv_sem, x_send_sem, x_recv_sem,
    px_send_sem, px_recv_sem, z_send_sem, z_recv_sem, ig_send_sem, ig_recv_sem,
):
    grp = lax.axis_index("grp")
    y = lax.axis_index("fsdp")
    core = lax.rem(grp, CORES)
    wide = lax.rem(grp // CORES, WIDE)
    z = grp // (CORES * WIDE)
    oy, oc = 1 - y, 1 - core
    tokens = s_hbm.shape[0]
    groups = mask_ref.shape[0]
    rows = wg_ref.shape[0]
    half = w_hbm.shape[0]

    def at(zz, xx, cc, yy):
        return ((zz * WIDE + xx) * CORES + cc, yy)

    def remote(src, dst, send, recv, device):
        copy = pltpu.make_async_remote_copy(
            src_ref=src, dst_ref=dst, send_sem=send, recv_sem=recv,
            device_id=device, device_id_type=MESH,
        )
        return copy

    y_peer = at(z, wide, core, oy)
    y_cross = at(z, wide, oc, oy)
    sibling = at(z, wide, oc, y)
    x_peer = at(z, 1 - wide, core, y)
    z_to = [at(lax.rem(z + k, deep), wide, core, y) for k in range(1, deep)]
    me = core * 2 + y
    from_y = core * 2 + oy
    from_cross = oc * 2 + oy
    from_sib = oc * 2 + y

    load_s = pltpu.make_async_copy(s_hbm, s_v.at[me], load_sem.at[0])
    load_x = pltpu.make_async_copy(x_hbm, x_v, load_sem.at[1])
    load_w = pltpu.make_async_copy(w_hbm, w_v, load_sem.at[2])
    load_s.start()
    load_x.start()
    load_w.start()

    barrier = pltpu.get_barrier_semaphore()
    partners = [y_peer, y_cross, sibling, x_peer] + z_to
    for partner in partners:
        pl.semaphore_signal(barrier, inc=1, device_id=partner, device_id_type=MESH)

    order = [k for k in range(1, deep)] + [0]
    span = WIDE * CORES * 2 * rows

    def turn(k):
        zz = lax.rem(z + k, deep)
        part = x_v[:, pl.ds(pl.multiple_of(zz * span, span), span)].T
        for xx in range(WIDE):
            for cy in range(CORES * 2):
                start = (xx * CORES * 2 + cy) * rows
                tx[k, cy, xx * rows:(xx + 1) * rows, :] = part[start:start + rows, :]

    load_x.wait()
    turn(order[0])
    load_s.wait()
    pl.semaphore_wait(barrier, len(partners))

    s_y = remote(s_v.at[me], s_v.at[me], s_send_sem.at[0], s_recv_sem.at[0], y_peer)
    s_sib = remote(s_v.at[me], s_v.at[me], s_send_sem.at[1], s_recv_sem.at[1], sibling)
    s_fwd = remote(s_v.at[from_y], s_v.at[from_y], s_send_sem.at[2], s_recv_sem.at[2], sibling)
    s_y.start()
    s_sib.start()

    x_copies = {}
    for n, k in enumerate(order):
        if n:
            turn(k)
        copies = []
        for slot, (device, there) in enumerate(
            ((y_peer, from_y), (y_cross, from_cross), (sibling, from_sib))
        ):
            copy = remote(
                tx.at[k, there], rx.at[k, me], x_send_sem.at[k, slot], x_recv_sem.at[k, slot], device
            )
            copy.start()
            copies.append(copy)
        x_copies[k] = copies
        rx[k, me] = tx[k, me]

    scales = []
    for cc in range(CORES):
        here = (z * WIDE + wide) * CORES + cc
        mine = list_ref[here]
        tally = jnp.int32(0)
        for h in range(groups):
            tally = tally + jnp.where(list_ref[h] == mine, mask_ref[h], 0)
        done = jnp.full((1, wg_ref.shape[1]), mask_ref[here], jnp.int32).astype(jnp.float32)
        total = jnp.full((1, wg_ref.shape[1]), tally, jnp.int32).astype(jnp.float32)
        scales.append(done / (total + 1.0 - done))

    load_w.wait()

    def grad(s_block):
        return lax.dot_general(
            s_block, w_v[...], (((1,), (1,)), ((), ())), preferred_element_type=jnp.float32
        ).astype(jnp.bfloat16)

    own_columns = pl.ds(pl.multiple_of(y * half, half), half)
    ig_ref[:, own_columns] = grad(s_v[me])

    s_y.wait_recv()
    s_fwd.start()
    ig_send[...] = grad(s_v[from_y])
    ig_copy = remote(ig_send, ig_ref.at[:, own_columns], ig_send_sem, ig_recv_sem, y_peer)
    ig_copy.start()

    s_sib.wait_recv()
    s_fwd.wait_recv()

    px_copies, z_copies = {}, {}

    def partial(k):
        for copy in x_copies[k]:
            copy.wait_recv()
        total = None
        for cc in range(CORES):
            left = jnp.concatenate([rx[k, cc * 2], rx[k, cc * 2 + 1]], axis=1)
            right = s_v[cc * 2:cc * 2 + 2].reshape(2 * tokens, s_v.shape[2])
            product = scales[cc] * jnp.dot(left, right, preferred_element_type=jnp.float32)
            total = product if total is None else total + product
        own_part[k, 0] = total[:rows]
        own_part[k, 1] = total[rows:]
        coded, scale = encode(own_part[k, 1 - wide])
        px_send[k] = coded
        px_scale[k] = scale

    def send_x(k):
        copies = [
            remote(px_send.at[k], px_recv.at[k], px_send_sem.at[k, 0], px_recv_sem.at[k, 0], x_peer),
            remote(px_scale.at[k], px_rscale.at[k], px_send_sem.at[k, 1], px_recv_sem.at[k, 1], x_peer),
        ]
        for copy in copies:
            copy.start()
        px_copies[k] = copies

    def gather_x(k):
        for copy in px_copies[k]:
            copy.wait_recv()
        value = own_part[k, wide] + decoded(px_recv[k], px_rscale[k])
        if k:
            coded, scale = encode(value)
            q_send[k] = coded
            q_scale[k] = scale
            copies = [
                remote(q_send.at[k], zr.at[k], z_send_sem.at[k, 0], z_recv_sem.at[k, 0], z_to[k - 1]),
                remote(q_scale.at[k], zr_scale.at[k], z_send_sem.at[k, 1], z_recv_sem.at[k, 1], z_to[k - 1]),
            ]
            for copy in copies:
                copy.start()
            z_copies[k] = copies
        else:
            q[...] = value

    for n, k in enumerate(order):
        partial(k)
        send_x(k)
        if n:
            gather_x(order[n - 1])
    gather_x(order[-1])

    total = q[...]
    for k in range(1, deep):
        for copy in z_copies[k]:
            copy.wait_recv()
        total = total + decoded(zr[k], zr_scale[k])
    wg_ref[...] = total

    ig_copy.wait_recv()

    for copy in (s_y, s_sib, s_fwd, ig_copy):
        copy.wait_send()
    for group in (x_copies, px_copies, z_copies):
        for copies in group.values():
            for copy in copies:
                copy.wait_send()


def kernel_shards(deep, rows, x, s, w, mask, plist):
    tokens, width = x.shape
    values = s.shape[1]
    f32, bf16, i16 = jnp.float32, jnp.bfloat16, jnp.int16
    dma = pltpu.SemaphoreType.DMA
    anywhere = pl.BlockSpec(memory_space=pl.ANY)
    smem = pl.BlockSpec(memory_space=pltpu.SMEM)
    wide_rows = WIDE * rows
    return pl.pallas_call(
        functools.partial(kernel, deep),
        out_shape=(
            pltpu.VMEM((tokens, width), bf16),
            pltpu.VMEM((rows, values), f32),
        ),
        in_specs=[smem, smem, anywhere, anywhere, anywhere],
        out_specs=(pl.BlockSpec(memory_space=pltpu.VMEM),) * 2,
        scratch_shapes=[
            pltpu.VMEM((tokens, width), bf16),
            pltpu.VMEM((CORES * 2, tokens, values), bf16),
            pltpu.VMEM(w.shape, bf16),
            pltpu.VMEM((deep, CORES * 2, wide_rows, tokens), bf16),
            pltpu.VMEM((deep, CORES * 2, wide_rows, tokens), bf16),
            pltpu.VMEM((deep, WIDE, rows, values), f32),
            pltpu.VMEM((deep, rows, values), i16),
            pltpu.VMEM((deep, 1, values), f32),
            pltpu.VMEM((deep, rows, values), i16),
            pltpu.VMEM((deep, 1, values), f32),
            pltpu.VMEM((rows, values), f32),
            pltpu.VMEM((deep, rows, values), i16),
            pltpu.VMEM((deep, 1, values), f32),
            pltpu.VMEM((deep, rows, values), i16),
            pltpu.VMEM((deep, 1, values), f32),
            pltpu.VMEM((tokens, w.shape[0]), bf16),
            dma((3,)), dma((3,)), dma((3,)), dma((deep, 3)), dma((deep, 3)),
            dma((deep, 2)), dma((deep, 2)), dma((deep, 2)), dma((deep, 2)), dma, dma,
        ],
        compiler_params=pltpu.CompilerParams(collective_id=0, has_side_effects=True),
    )(mask, plist, x, s, w)


def solution(mesh):
    outer, inner = mesh.shape["grp"], mesh.shape["fsdp"]

    def shards(x, s, w, mask, plist):
        rows = x.shape[1] // (outer * inner)
        if inner == 2 and outer % (CORES * WIDE) == 0 and rows % 16 == 0 and x.shape[0] % 128 == 0:
            return tuple(kernel_shards(outer // (CORES * WIDE), rows, x, s, w, mask, plist))
        return collective_shards(x, s, w, mask, plist)

    in_specs = (P(("grp", "fsdp"), None), P(("grp", "fsdp"), None), P("fsdp", None), P(), P())
    out_specs = (P(("grp", "fsdp"), None), P(("grp", "fsdp"), None))
    return jax.shard_map(shards, mesh=mesh, in_specs=in_specs, out_specs=out_specs, check_vma=False)
```

profile of v0, /device:TPU:0, one launch (start us, length us, event | category | flops | bytes accessed | tf_op | source)
XLA Modules:
  0.0 27.2 jit_solution(10229647971946853585)
XLA Ops:
  0.6 25.1 %shard_map.68 = (bf16[128,2048]{1,0:T(8,128)(2,1)S(1)}, f32[64,512]{1,0:T(8,128)S(1)}) custom-call(s32[16]{0:T(128)} %mask_ref.1, s32[16]{0:T(128)} %list_ref.1, bf16[128,2048]{1,0:T(8,128)(2,1)} %x_hbm.1, bf16[128,512]{1,0:T(8,128)(2,1)} %s_hbm.1, bf16[1024,512]{1,0:T(8,128)(2,1)} %w_hbm.1), custom_call_target="tpu_custom_call" | custom-call | tf_op jit(solution)/shard_map/pallas_call | solution.py:263
  25.7 0.8 %copy.9 = bf16[128,2048]{1,0:T(8,128)(2,1)} copy(bf16[128,2048]{1,0:T(8,128)(2,1)S(1)} %get-tuple-element.2) | data formatting | bytes 1048576
  26.5 0.7 %copy.10 = f32[64,512]{1,0:T(8,128)} copy(f32[64,512]{1,0:T(8,128)S(1)} %get-tuple-element.3) | data formatting | bytes 262144
where the time goes:
time: 27.3 us; the launch traced here: 27.2 us
  Pallas kernels  25.1 us (92%)
  local copies, waits for them, and re-layouts  1.45 us (5%)
  between operations  0.64 us (2%)
    pallas_call x1, Pallas kernels, kernel_shards(): pl.pallas_call(functools.partial(kernel, deep), out_shape=(pltpu.VMEM((to...  25.1 us
    unnamed x2, local copies, waits for them, and re-layouts  1.45 us

commit v1 on v0

v1 whole, which is shorter than its diff:
```python
import functools

import jax
import jax.numpy as jnp
from jax import lax
from jax.experimental import pallas as pl
from jax.experimental.pallas import tpu as pltpu
from jax.sharding import PartitionSpec as P

MESH = pl.DeviceIdType.MESH
CORES = 2
WIDE = 2
STEPS = 32766.0
TINY = 1e-33


def collective_shards(
    normalized_inputs,
    output_sensitivity,
    projection_weights,
    completion_mask,
    replica_partition_list,
):
    replica_index = lax.axis_index("grp")
    selected_replica = lax.iota(jnp.int32, completion_mask.shape[0]) == replica_index
    assigned_piece = jnp.sum(jnp.where(selected_replica, replica_partition_list, 0))
    finished_indicator = jnp.sum(jnp.where(selected_replica, completion_mask, 0))
    finisher_tally = jnp.sum(
        jnp.where(replica_partition_list == assigned_piece, completion_mask, 0)
    )
    living_float = finished_indicator.astype(jnp.float32)
    decode_sum = living_float / (finisher_tally.astype(jnp.float32) + 1.0 - living_float)
    tokens_here = normalized_inputs.shape[0]
    model_width = normalized_inputs.shape[1]
    inner_size = lax.axis_size("fsdp")
    outer_size = lax.axis_size("grp")
    input_grad = lax.dot_general(
        output_sensitivity,
        lax.all_gather(projection_weights, "fsdp", axis=0, tiled=True),
        (((1,), (1,)), ((), ())),
        preferred_element_type=jnp.float32,
    ).astype(jnp.bfloat16)
    owner_rows = model_width // (outer_size * inner_size)
    reordered = normalized_inputs.reshape(tokens_here, outer_size, inner_size, owner_rows)
    reordered = reordered.transpose(0, 2, 1, 3).reshape(tokens_here, model_width)
    column_block = lax.all_to_all(reordered, "fsdp", split_axis=1, concat_axis=0, tiled=True)
    group_block = lax.dot_general(
        column_block,
        lax.all_gather(output_sensitivity, "fsdp", axis=0, tiled=True),
        (((0,), (0,)), ((), ())),
        preferred_element_type=jnp.float32,
    )
    weight_grad = lax.psum_scatter(decode_sum * group_block, "grp", scatter_dimension=0, tiled=True)
    return (input_grad, weight_grad)


def encode(value):
    top = jnp.maximum(jnp.max(jnp.abs(value), axis=0, keepdims=True), TINY)
    coded = jnp.round(value * (STEPS / top)).astype(jnp.int32).astype(jnp.int16)
    return coded, top * (1.0 / STEPS)


def decoded(coded, step):
    return coded.astype(jnp.int32).astype(jnp.float32) * step


def kernel(
    deep,
    mask_hbm, list_hbm, x_hbm, s_hbm, w_hbm,
    ig_ref, wg_ref,
    mask_ref, list_ref,
    x_v, s_v, w_v, tx, rx, own_part, px_send, px_scale, px_recv, px_rscale,
    q, q_send, q_scale, zr, zr_scale, ig_send,
    load_sem, s_send_sem, s_recv_sem, x_send_sem, x_recv_sem,
    px_send_sem, px_recv_sem, z_send_sem, z_recv_sem, ig_send_sem, ig_recv_sem, hello,
):
    grp = lax.axis_index("grp")
    y = lax.axis_index("fsdp")
    core = lax.rem(grp, CORES)
    wide = lax.rem(grp // CORES, WIDE)
    z = grp // (CORES * WIDE)
    oy, oc = 1 - y, 1 - core
    tokens = s_hbm.shape[0]
    groups = mask_ref.shape[0]
    rows = wg_ref.shape[0]
    half = w_hbm.shape[0]
    part_tokens = tokens // 2

    def at(zz, xx, cc, yy):
        return ((zz * WIDE + xx) * CORES + cc, yy)

    def remote(src, dst, send, recv, device):
        return pltpu.make_async_remote_copy(
            src_ref=src, dst_ref=dst, send_sem=send, recv_sem=recv,
            device_id=device, device_id_type=MESH,
        )

    y_peer = at(z, wide, core, oy)
    y_cross = at(z, wide, oc, oy)
    sibling = at(z, wide, oc, y)
    x_peer = at(z, 1 - wide, core, y)
    below = at(lax.rem(z + deep - 1, deep), wide, core, y)
    above = at(lax.rem(z + 1, deep), wide, core, y)
    me = core * 2 + y
    from_y = core * 2 + oy
    from_cross = oc * 2 + oy
    from_sib = oc * 2 + y

    barrier = pltpu.get_barrier_semaphore()
    partners = [y_peer, y_cross, sibling, x_peer]
    for partner in partners:
        pl.semaphore_signal(barrier, inc=1, device_id=partner, device_id_type=MESH)

    @pl.when(z > 0)
    def _():
        pl.semaphore_signal(barrier, inc=1, device_id=below, device_id_type=MESH)

    @pl.when(z < deep - 1)
    def _():
        pl.semaphore_signal(barrier, inc=1, device_id=above, device_id_type=MESH)

    load_x = pltpu.make_async_copy(x_hbm, x_v, load_sem.at[0])
    load_s = pltpu.make_async_copy(s_hbm, s_v.at[me], load_sem.at[1])
    load_w = pltpu.make_async_copy(w_hbm, w_v, load_sem.at[2])
    load_mask = pltpu.make_async_copy(mask_hbm, mask_ref, load_sem.at[3])
    load_list = pltpu.make_async_copy(list_hbm, list_ref, load_sem.at[4])
    loads = [load_x, load_s, load_w, load_mask, load_list]
    for load in loads:
        load.start()

    first, second = pl.ds(0, part_tokens), pl.ds(part_tokens, part_tokens)
    s_y = remote(s_hbm.at[first], s_v.at[me, first], s_send_sem.at[0], s_recv_sem.at[0], y_peer)
    s_cross = remote(s_hbm.at[second], s_v.at[me, second], s_send_sem.at[1], s_recv_sem.at[1], y_cross)
    s_sib = remote(s_hbm, s_v.at[me], s_send_sem.at[2], s_recv_sem.at[2], sibling)
    forward_y = remote(
        s_v.at[from_y, first], s_v.at[from_y, first], s_send_sem.at[3], s_recv_sem.at[3], sibling
    )
    forward_cross = remote(
        s_v.at[from_cross, second], s_v.at[from_cross, second], s_send_sem.at[4], s_recv_sem.at[4], sibling
    )

    @pl.when(jnp.logical_and(z > 0, z < deep - 1))
    def _():
        pl.semaphore_wait(barrier, len(partners) + 2)

    @pl.when(jnp.logical_or(z == 0, z == deep - 1))
    def _():
        pl.semaphore_wait(barrier, len(partners) + 1)

    s_y.start()
    s_cross.start()
    s_sib.start()

    @pl.when(z == deep - 2)
    def _():
        pl.semaphore_signal(hello.at[0], inc=1, device_id=below, device_id_type=MESH)

    @pl.when(z == 1)
    def _():
        pl.semaphore_signal(hello.at[1], inc=1, device_id=above, device_id_type=MESH)

    span = WIDE * CORES * 2 * rows

    def plane(n):
        if n == deep - 1:
            return z
        return jnp.where(z == 0, deep - 1 - n, jnp.where(n < z, n, n + 1))

    def turn(n):
        part = x_v[:, pl.ds(pl.multiple_of(plane(n) * span, span), span)].T
        for xx in range(WIDE):
            for cy in range(CORES * 2):
                start = (xx * CORES * 2 + cy) * rows
                tx[n, cy, xx * rows:(xx + 1) * rows, :] = part[start:start + rows, :]

    load_x.wait()
    x_copies = []
    for n in range(deep):
        turn(n)
        p = plane(n)
        copies = []
        for slot, (device, there) in enumerate(
            ((y_peer, from_y), (y_cross, from_cross), (sibling, from_sib))
        ):
            copy = remote(
                tx.at[n, there], rx.at[n, me], x_send_sem.at[n, slot], x_recv_sem.at[n, slot], device
            )
            copy.start()
            copies.append(copy)
        x_copies.append(copies)
        rx[n, me] = tx[n, me]

    load_mask.wait()
    load_list.wait()
    scales = []
    for cc in range(CORES):
        here = (z * WIDE + wide) * CORES + cc
        mine = list_ref[here]
        tally = jnp.int32(0)
        for h in range(groups):
            tally = tally + jnp.where(list_ref[h] == mine, mask_ref[h], 0)
        done = jnp.full((1, wg_ref.shape[1]), mask_ref[here], jnp.int32).astype(jnp.float32)
        total = jnp.full((1, wg_ref.shape[1]), tally, jnp.int32).astype(jnp.float32)
        scales.append(done / (total + 1.0 - done))

    load_s.wait()
    load_w.wait()

    def grad(s_block):
        return lax.dot_general(
            s_block, w_v[...], (((1,), (1,)), ((), ())), preferred_element_type=jnp.float32
        ).astype(jnp.bfloat16)

    own_columns = pl.ds(pl.multiple_of(y * half, half), half)
    ig_ref[:, own_columns] = grad(s_v[me])

    s_y.wait_recv()
    forward_y.start()
    s_cross.wait_recv()
    forward_cross.start()
    ig_send[...] = grad(jnp.concatenate([s_v[from_y, first], s_v[from_cross, second]], axis=0))
    ig_y = remote(ig_send.at[first], ig_ref.at[first, own_columns], ig_send_sem.at[0], ig_recv_sem.at[0], y_peer)
    ig_cross = remote(
        ig_send.at[second], ig_ref.at[second, own_columns], ig_send_sem.at[1], ig_recv_sem.at[1], y_cross
    )
    ig_y.start()
    ig_cross.start()

    @pl.when(jnp.logical_and(z > 0, z < deep - 2))
    def _():
        pl.semaphore_wait(hello.at[0], 1)
        pl.semaphore_signal(hello.at[0], inc=1, device_id=below, device_id_type=MESH)

    @pl.when(jnp.logical_and(z > 1, z < deep - 1))
    def _():
        pl.semaphore_wait(hello.at[1], 1)
        pl.semaphore_signal(hello.at[1], inc=1, device_id=above, device_id_type=MESH)

    s_sib.wait_recv()
    forward_y.wait_recv()
    forward_cross.wait_recv()

    px_copies, z_copies = {}, {}

    def partial(n):
        for copy in x_copies[n]:
            copy.wait_recv()
        total = None
        for cc in range(CORES):
            left = jnp.concatenate([rx[n, cc * 2], rx[n, cc * 2 + 1]], axis=1)
            right = s_v[cc * 2:cc * 2 + 2].reshape(2 * tokens, s_v.shape[2])
            product = scales[cc] * jnp.dot(left, right, preferred_element_type=jnp.float32)
            total = product if total is None else total + product
        own_part[n, 0] = total[:rows]
        own_part[n, 1] = total[rows:]
        coded, scale = encode(own_part[n, 1 - wide])
        px_send[n] = coded
        px_scale[n] = scale

    def send_x(n):
        copies = [
            remote(px_send.at[n], px_recv.at[n], px_send_sem.at[n, 0], px_recv_sem.at[n, 0], x_peer),
            remote(px_scale.at[n], px_rscale.at[n], px_send_sem.at[n, 1], px_recv_sem.at[n, 1], x_peer),
        ]
        for copy in copies:
            copy.start()
        px_copies[n] = copies

    def gather_x(n):
        for copy in px_copies[n]:
            copy.wait_recv()
        value = own_part[n, wide] + decoded(px_recv[n], px_rscale[n])
        if n < deep - 1:
            coded, scale = encode(value)
            q_send[n] = coded
            q_scale[n] = scale
            there = at(plane(n), wide, core, y)
            copies = [
                remote(q_send.at[n], zr.at[z], z_send_sem.at[n, 0], z_recv_sem.at[z, 0], there),
                remote(q_scale.at[n], zr_scale.at[z], z_send_sem.at[n, 1], z_recv_sem.at[z, 1], there),
            ]
            for copy in copies:
                copy.start()
            z_copies[n] = copies
        else:
            q[...] = value

    for n in range(deep):
        partial(n)
        send_x(n)
        if n == 1:
            @pl.when(z == 0)
            def _():
                pl.semaphore_wait(hello.at[0], 1)

            @pl.when(z == deep - 1)
            def _():
                pl.semaphore_wait(hello.at[1], 1)
        if n:
            gather_x(n - 1)
    gather_x(deep - 1)

    total = q[...]
    for n in range(deep - 1):
        source = jnp.where(n < z, n, n + 1)
        for piece, part in enumerate((zr, zr_scale)):
            remote(
                part.at[source], part.at[source], z_send_sem.at[n, piece], z_recv_sem.at[source, piece], sibling
            ).wait_recv()
        total = total + decoded(zr[source], zr_scale[source])
    wg_ref[...] = total

    ig_y.wait_recv()
    ig_cross.wait_recv()

    for copy in (s_y, s_cross, s_sib, forward_y, forward_cross, ig_y, ig_cross):
        copy.wait_send()
    for group in (x_copies, px_copies.values(), z_copies.values()):
        for copies in group:
            for copy in copies:
                copy.wait_send()


def kernel_shards(deep, rows, x, s, w, mask, plist):
    tokens, width = x.shape
    values = s.shape[1]
    f32, bf16, i16 = jnp.float32, jnp.bfloat16, jnp.int16
    dma = pltpu.SemaphoreType.DMA
    anywhere = pl.BlockSpec(memory_space=pl.ANY)
    wide_rows = WIDE * rows
    return pl.pallas_call(
        functools.partial(kernel, deep),
        out_shape=(
            pltpu.VMEM((tokens, width), bf16),
            pltpu.VMEM((rows, values), f32),
        ),
        in_specs=[anywhere] * 5,
        out_specs=(pl.BlockSpec(memory_space=pltpu.VMEM),) * 2,
        scratch_shapes=[
            pltpu.SMEM(mask.shape, jnp.int32),
            pltpu.SMEM(plist.shape, jnp.int32),
            pltpu.VMEM((tokens, width), bf16),
            pltpu.VMEM((CORES * 2, tokens, values), bf16),
            pltpu.VMEM(w.shape, bf16),
            pltpu.VMEM((deep, CORES * 2, wide_rows, tokens), bf16),
            pltpu.VMEM((deep, CORES * 2, wide_rows, tokens), bf16),
            pltpu.VMEM((deep, WIDE, rows, values), f32),
            pltpu.VMEM((deep, rows, values), i16),
            pltpu.VMEM((deep, 1, values), f32),
            pltpu.VMEM((deep, rows, values), i16),
            pltpu.VMEM((deep, 1, values), f32),
            pltpu.VMEM((rows, values), f32),
            pltpu.VMEM((deep, rows, values), i16),
            pltpu.VMEM((deep, 1, values), f32),
            pltpu.VMEM((deep, rows, values), i16),
            pltpu.VMEM((deep, 1, values), f32),
            pltpu.VMEM((tokens, w.shape[0]), bf16),
            dma((5,)), dma((5,)), dma((5,)), dma((deep, 3)), dma((deep, 3)),
            dma((deep, 2)), dma((deep, 2)), dma((deep, 2)), dma((deep, 2)), dma((2,)), dma((2,)),
            pltpu.SemaphoreType.REGULAR((2,)),
        ],
        compiler_params=pltpu.CompilerParams(collective_id=0, has_side_effects=True),
    )(mask, plist, x, s, w)


def solution(mesh):
    outer, inner = mesh.shape["grp"], mesh.shape["fsdp"]

    def shards(x, s, w, mask, plist):
        rows = x.shape[1] // (outer * inner)
        if inner == 2 and outer % (CORES * WIDE) == 0 and outer // (CORES * WIDE) >= 4 and rows % 16 == 0 and x.shape[0] % 128 == 0:
            return tuple(kernel_shards(outer // (CORES * WIDE), rows, x, s, w, mask, plist))
        return collective_shards(x, s, w, mask, plist)

    in_specs = (P(("grp", "fsdp"), None), P(("grp", "fsdp"), None), P("fsdp", None), P(), P())
    out_specs = (P(("grp", "fsdp"), None), P(("grp", "fsdp"), None))
    return jax.shard_map(shards, mesh=mesh, in_specs=in_specs, out_specs=out_specs, check_vma=False)
```

time: 27.3 us -> 25.8 us (0.945)
  Pallas kernels: 25.1 us -> 23.5 us
    pallas_call x1, Pallas kernels: 25.1 us -> 23.5 us  [kernel_shards(): pl.pallas_call(functools.partial(kernel, deep), out_shape=(pltpu.VMEM((to...]
where the time goes in v1:
time: 25.8 us; the launch traced here: 25.6 us
  Pallas kernels  23.5 us (91%)
  local copies, waits for them, and re-layouts  1.45 us (6%)
  between operations  0.64 us (2%)
    pallas_call x1, Pallas kernels, kernel_shards(): pl.pallas_call(functools.partial(kernel, deep), out_shape=(pltpu.VMEM((to...  23.5 us
    unnamed x2, local copies, waits for them, and re-layouts  1.45 us

profile of v1, /device:TPU:0, one launch (start us, length us, event | category | flops | bytes accessed | tf_op | source)
XLA Modules:
  0.0 25.6 jit_solution(7980408052108614972)
XLA Ops:
  0.6 23.5 %shard_map.68 = (bf16[128,2048]{1,0:T(8,128)(2,1)S(1)}, f32[64,512]{1,0:T(8,128)S(1)}) custom-call(s32[16]{0:T(128)} %mask_hbm.1, s32[16]{0:T(128)} %list_hbm.1, bf16[128,2048]{1,0:T(8,128)(2,1)} %x_hbm.1, bf16[128,512]{1,0:T(8,128)(2,1)} %s_hbm.1, bf16[1024,512]{1,0:T(8,128)(2,1)} %w_hbm.1), custom_call_target="tpu_custom_call" | custom-call | tf_op jit(solution)/shard_map/pallas_call | solution.py:331
  24.2 0.8 %copy.9 = bf16[128,2048]{1,0:T(8,128)(2,1)} copy(bf16[128,2048]{1,0:T(8,128)(2,1)S(1)} %get-tuple-element.2) | data formatting | bytes 1048576
  25.0 0.7 %copy.10 = f32[64,512]{1,0:T(8,128)} copy(f32[64,512]{1,0:T(8,128)S(1)} %get-tuple-element.3) | data formatting | bytes 262144

commit v2 on v1

--- a/solution.py
+++ b/solution.py
@@ -10,6 +10,9 @@
 MESH = pl.DeviceIdType.MESH
 CORES = 2
 WIDE = 2
+HALVES = 2
+LAG = 2
+SMALL = 1 << 20
 STEPS = 32766.0
 TINY = 1e-33
 
@@ -85,6 +88,8 @@
     rows = wg_ref.shape[0]
     half = w_hbm.shape[0]
     part_tokens = tokens // 2
+    part_rows = rows // HALVES
+    pieces = deep * HALVES
 
     def at(zz, xx, cc, yy):
         return ((zz * WIDE + xx) * CORES + cc, yy)
@@ -129,14 +134,18 @@
         load.start()
 
     first, second = pl.ds(0, part_tokens), pl.ds(part_tokens, part_tokens)
-    s_y = remote(s_hbm.at[first], s_v.at[me, first], s_send_sem.at[0], s_recv_sem.at[0], y_peer)
-    s_cross = remote(s_hbm.at[second], s_v.at[me, second], s_send_sem.at[1], s_recv_sem.at[1], y_cross)
-    s_sib = remote(s_hbm, s_v.at[me], s_send_sem.at[2], s_recv_sem.at[2], sibling)
-    forward_y = remote(
-        s_v.at[from_y, first], s_v.at[from_y, first], s_send_sem.at[3], s_recv_sem.at[3], sibling
-    )
+    def received(ref, sem):
+        remote(ref, ref, sem, sem, sibling).wait_recv()
+
+    def sent(ref, sem):
+        remote(ref, ref, sem, sem, sibling).wait_send()
+
+    s_y = remote(s_hbm.at[first], s_v.at[me, first], s_send_sem, s_recv_sem.at[0], y_peer)
+    s_cross = remote(s_hbm.at[second], s_v.at[me, second], s_send_sem, s_recv_sem.at[0], y_cross)
+    s_sib = remote(s_hbm, s_v.at[me], s_send_sem, s_recv_sem.at[1], sibling)
+    forward_y = remote(s_v.at[from_y, first], s_v.at[from_y, first], s_send_sem, s_recv_sem.at[1], sibling)
     forward_cross = remote(
-        s_v.at[from_cross, second], s_v.at[from_cross, second], s_send_sem.at[4], s_recv_sem.at[4], sibling
+        s_v.at[from_cross, second], s_v.at[from_cross, second], s_send_sem, s_recv_sem.at[1], sibling
     )
 
     @pl.when(jnp.logical_and(z > 0, z < deep - 1))
@@ -164,31 +173,24 @@
     def plane(n):
         if n == deep - 1:
             return z
-        return jnp.where(z == 0, deep - 1 - n, jnp.where(n < z, n, n + 1))
+        down = jnp.where(deep - 1 - n > z, deep - 1 - n, deep - 2 - n)
+        return jnp.where(z < deep // 2, down, jnp.where(n < z, n, n + 1))
 
     def turn(n):
         part = x_v[:, pl.ds(pl.multiple_of(plane(n) * span, span), span)].T
         for xx in range(WIDE):
             for cy in range(CORES * 2):
-                start = (xx * CORES * 2 + cy) * rows
-                tx[n, cy, xx * rows:(xx + 1) * rows, :] = part[start:start + rows, :]
+                for h in range(HALVES):
+                    start = (xx * CORES * 2 + cy) * rows + h * part_rows
+                    tx[n * HALVES + h, cy, xx * part_rows:(xx + 1) * part_rows, :] = part[start:start + part_rows, :]
 
     load_x.wait()
-    x_copies = []
     for n in range(deep):
         turn(n)
-        p = plane(n)
-        copies = []
-        for slot, (device, there) in enumerate(
-            ((y_peer, from_y), (y_cross, from_cross), (sibling, from_sib))
-        ):
-            copy = remote(
-                tx.at[n, there], rx.at[n, me], x_send_sem.at[n, slot], x_recv_sem.at[n, slot], device
-            )
-            copy.start()
-            copies.append(copy)
-        x_copies.append(copies)
-        rx[n, me] = tx[n, me]
+        for j in range(n * HALVES, (n + 1) * HALVES):
+            for device, there in ((y_peer, from_y), (y_cross, from_cross), (sibling, from_sib)):
+                remote(tx.at[j, there], rx.at[j, me], x_send_sem, x_recv_sem.at[j], device).start()
+            rx[j, me] = tx[j, me]
 
     load_mask.wait()
     load_list.wait()
@@ -214,17 +216,12 @@
     own_columns = pl.ds(pl.multiple_of(y * half, half), half)
     ig_ref[:, own_columns] = grad(s_v[me])
 
-    s_y.wait_recv()
+    received(s_v.at[me], s_recv_sem.at[0])
     forward_y.start()
-    s_cross.wait_recv()
     forward_cross.start()
     ig_send[...] = grad(jnp.concatenate([s_v[from_y, first], s_v[from_cross, second]], axis=0))
-    ig_y = remote(ig_send.at[first], ig_ref.at[first, own_columns], ig_send_sem.at[0], ig_recv_sem.at[0], y_peer)
-    ig_cross = remote(
-        ig_send.at[second], ig_ref.at[second, own_columns], ig_send_sem.at[1], ig_recv_sem.at[1], y_cross
-    )
-    ig_y.start()
-    ig_cross.start()
+    remote(ig_send.at[first], ig_ref.at[first, own_columns], ig_send_sem, ig_recv_sem, y_peer).start()
+    remote(ig_send.at[second], ig_ref.at[second, own_columns], ig_send_sem, ig_recv_sem, y_cross).start()
 
     @pl.when(jnp.logical_and(z > 0, z < deep - 2))
     def _():
@@ -236,59 +233,27 @@
         pl.semaphore_wait(hello.at[1], 1)
         pl.semaphore_signal(hello.at[1], inc=1, device_id=above, device_id_type=MESH)
 
-    s_sib.wait_recv()
-    forward_y.wait_recv()
-    forward_cross.wait_recv()
-
-    px_copies, z_copies = {}, {}
-
-    def partial(n):
-        for copy in x_copies[n]:
-            copy.wait_recv()
+    received(s_v.at[0:2], s_recv_sem.at[1])
+
+    def partial(j):
+        received(rx.at[j, 0:3], x_recv_sem.at[j])
         total = None
         for cc in range(CORES):
-            left = jnp.concatenate([rx[n, cc * 2], rx[n, cc * 2 + 1]], axis=1)
+            left = jnp.concatenate([rx[j, cc * 2], rx[j, cc * 2 + 1]], axis=1)
             right = s_v[cc * 2:cc * 2 + 2].reshape(2 * tokens, s_v.shape[2])
             product = scales[cc] * jnp.dot(left, right, preferred_element_type=jnp.float32)
             total = product if total is None else total + product
-        own_part[n, 0] = total[:rows]
-        own_part[n, 1] = total[rows:]
-        coded, scale = encode(own_part[n, 1 - wide])
-        px_send[n] = coded
-        px_scale[n] = scale
-
-    def send_x(n):
-        copies = [
-            remote(px_send.at[n], px_recv.at[n], px_send_sem.at[n, 0], px_recv_sem.at[n, 0], x_peer),
-            remote(px_scale.at[n], px_rscale.at[n], px_send_sem.at[n, 1], px_recv_sem.at[n, 1], x_peer),
-        ]
-        for copy in copies:
-            copy.start()
-        px_copies[n] = copies
-
-    def gather_x(n):
-        for copy in px_copies[n]:
-            copy.wait_recv()
-        value = own_part[n, wide] + decoded(px_recv[n], px_rscale[n])
-        if n < deep - 1:
-            coded, scale = encode(value)
-            q_send[n] = coded
-            q_scale[n] = scale
-            there = at(plane(n), wide, core, y)
-            copies = [
-                remote(q_send.at[n], zr.at[z], z_send_sem.at[n, 0], z_recv_sem.at[z, 0], there),
-                remote(q_scale.at[n], zr_scale.at[z], z_send_sem.at[n, 1], z_recv_sem.at[z, 1], there),
-            ]
-            for copy in copies:
-                copy.start()
-            z_copies[n] = copies
-        else:
-            q[...] = value
-
-    for n in range(deep):
-        partial(n)
-        send_x(n)
-        if n == 1:
+        own_part[j, 0] = total[:part_rows]
+        own_part[j, 1] = total[part_rows:]
+        coded, scale = encode(own_part[j, 1 - wide])
+        px_send[j] = coded
+        px_scale[j] = scale
+        remote(px_send.at[j], px_recv.at[j], px_send_sem.at[0], px_recv_sem.at[j, 0], x_peer).start()
+        remote(px_scale.at[j], px_rscale.at[j], px_send_sem.at[1], px_recv_sem.at[j, 1], x_peer).start()
+
+    def gather_x(j):
+        n, h = j // HALVES, j % HALVES
+        if j == 0:
             @pl.when(z == 0)
             def _():
                 pl.semaphore_wait(hello.at[0], 1)
@@ -296,29 +261,57 @@
             @pl.when(z == deep - 1)
             def _():
                 pl.semaphore_wait(hello.at[1], 1)
-        if n:
-            gather_x(n - 1)
-    gather_x(deep - 1)
-
-    total = q[...]
+
+        received(px_recv.at[j], px_recv_sem.at[j, 0])
+        received(px_rscale.at[j], px_recv_sem.at[j, 1])
+        value = own_part[j, wide] + decoded(px_recv[j], px_rscale[j])
+        if n < deep - 1:
+            coded, scale = encode(value)
+            q_send[j] = coded
+            q_scale[j] = scale
+            there = at(plane(n), wide, core, y)
+            remote(q_send.at[j], zr.at[z, h], z_send_sem.at[0], z_recv_sem.at[z, 0], there).start()
+            remote(q_scale.at[j], zr_scale.at[z, h], z_send_sem.at[1], z_recv_sem.at[z, 1], there).start()
+        else:
+            q[h] = value
+
+    for j in range(pieces + LAG):
+        if j < pieces:
+            partial(j)
+        if j >= LAG:
+            gather_x(j - LAG)
+
+    sent(s_v.at[0:3], s_send_sem)
+    sent(tx.at[:, 0:3], x_send_sem)
+    sent(px_send, px_send_sem.at[0])
+    sent(px_scale, px_send_sem.at[1])
+    sent(q_send, z_send_sem.at[0])
+    sent(q_scale, z_send_sem.at[1])
+    sent(ig_send, ig_send_sem)
+
     for n in range(deep - 1):
         source = jnp.where(n < z, n, n + 1)
-        for piece, part in enumerate((zr, zr_scale)):
-            remote(
-                part.at[source], part.at[source], z_send_sem.at[n, piece], z_recv_sem.at[source, piece], sibling
-            ).wait_recv()
-        total = total + decoded(zr[source], zr_scale[source])
-    wg_ref[...] = total
-
-    ig_y.wait_recv()
-    ig_cross.wait_recv()
-
-    for copy in (s_y, s_cross, s_sib, forward_y, forward_cross, ig_y, ig_cross):
-        copy.wait_send()
-    for group in (x_copies, px_copies.values(), z_copies.values()):
-        for copies in group:
-            for copy in copies:
-                copy.wait_send()
+        received(zr.at[source], z_recv_sem.at[source, 0])
+        received(zr_scale.at[source], z_recv_sem.at[source, 1])
+        for h in range(HALVES):
+            value = decoded(zr[source, h], zr_scale[source, h])
+            if n < deep - 2:
+                q[h] = q[h] + value
+            else:
+                wg_ref[h * part_rows:(h + 1) * part_rows, :] = q[h] + value
+
+    received(ig_send, ig_recv_sem)
+
+
+def write_out(ig_ref, wg_ref, ig_hbm, wg_hbm, sems):
+    copies = [
+        pltpu.make_async_copy(ig_ref, ig_hbm, sems.at[0]),
+        pltpu.make_async_copy(wg_ref, wg_hbm, sems.at[1]),
+    ]
+    for copy in copies:
+        copy.start()
+    for copy in copies:
+        copy.wait()
 
 
 def kernel_shards(deep, rows, x, s, w, mask, plist):
@@ -327,8 +320,8 @@
     f32, bf16, i16 = jnp.float32, jnp.bfloat16, jnp.int16
     dma = pltpu.SemaphoreType.DMA
     anywhere = pl.BlockSpec(memory_space=pl.ANY)
-    wide_rows = WIDE * rows
-    return pl.pallas_call(
+    part_rows, pieces = rows // HALVES, deep * HALVES
+    on_chip = pl.pallas_call(
         functools.partial(kernel, deep),
         out_shape=(
             pltpu.VMEM((tokens, width), bf16),
@@ -342,25 +335,36 @@
             pltpu.VMEM((tokens, width), bf16),
             pltpu.VMEM((CORES * 2, tokens, values), bf16),
             pltpu.VMEM(w.shape, bf16),
-            pltpu.VMEM((deep, CORES * 2, wide_rows, tokens), bf16),
-            pltpu.VMEM((deep, CORES * 2, wide_rows, tokens), bf16),
-            pltpu.VMEM((deep, WIDE, rows, values), f32),
-            pltpu.VMEM((deep, rows, values), i16),
-            pltpu.VMEM((deep, 1, values), f32),
-            pltpu.VMEM((deep, rows, values), i16),
-            pltpu.VMEM((deep, 1, values), f32),
-            pltpu.VMEM((rows, values), f32),
-            pltpu.VMEM((deep, rows, values), i16),
-            pltpu.VMEM((deep, 1, values), f32),
-            pltpu.VMEM((deep, rows, values), i16),
-            pltpu.VMEM((deep, 1, values), f32),
+            pltpu.VMEM((pieces, CORES * 2, WIDE * part_rows, tokens), bf16),
+            pltpu.VMEM((pieces, CORES * 2, WIDE * part_rows, tokens), bf16),
+            pltpu.VMEM((pieces, WIDE, part_rows, values), f32),
+            pltpu.VMEM((pieces, part_rows, values), i16),
+            pltpu.VMEM((pieces, 1, values), f32),
+            pltpu.VMEM((pieces, part_rows, values), i16),
+            pltpu.VMEM((pieces, 1, values), f32),
+            pltpu.VMEM((HALVES, part_rows, values), f32),
+            pltpu.VMEM((pieces - HALVES, part_rows, values), i16),
+            pltpu.VMEM((pieces - HALVES, 1, values), f32),
+            pltpu.VMEM((deep, HALVES, part_rows, values), i16),
+            pltpu.VMEM((deep, HALVES, 1, values), f32),
             pltpu.VMEM((tokens, w.shape[0]), bf16),
-            dma((5,)), dma((5,)), dma((5,)), dma((deep, 3)), dma((deep, 3)),
-            dma((deep, 2)), dma((deep, 2)), dma((deep, 2)), dma((deep, 2)), dma((2,)), dma((2,)),
+            dma((5,)), dma, dma((2,)), dma, dma((pieces,)),
+            dma((2,)), dma((pieces, 2)), dma((2,)), dma((deep, 2)), dma, dma,
             pltpu.SemaphoreType.REGULAR((2,)),
         ],
         compiler_params=pltpu.CompilerParams(collective_id=0, has_side_effects=True),
     )(mask, plist, x, s, w)
+    return pl.pallas_call(
+        write_out,
+        out_shape=(
+            jax.ShapeDtypeStruct((tokens, width), bf16),
+            jax.ShapeDtypeStruct((rows, values), f32),
+        ),
+        in_specs=[pl.BlockSpec(memory_space=pltpu.VMEM)] * 2,
+        out_specs=(anywhere,) * 2,
+        scratch_shapes=[dma((2,))],
+        compiler_params=pltpu.CompilerParams(vmem_limit_bytes=SMALL),
+    )(*(pltpu.with_memory_space_constraint(part, pltpu.VMEM) for part in on_chip))
 
 
 def solution(mesh):
@@ -368,7 +372,7 @@
 
     def shards(x, s, w, mask, plist):
         rows = x.shape[1] // (outer * inner)
-        if inner == 2 and outer % (CORES * WIDE) == 0 and outer // (CORES * WIDE) >= 4 and rows % 16 == 0 and x.shape[0] % 128 == 0:
+        if inner == 2 and outer % (CORES * WIDE) == 0 and outer // (CORES * WIDE) >= 4 and rows % (16 * HALVES) == 0 and x.shape[0] % 128 == 0:
             return tuple(kernel_shards(outer // (CORES * WIDE), rows, x, s, w, mask, plist))
         return collective_shards(x, s, w, mask, plist)
 

time: 25.8 us -> 23.8 us (0.922)
  local copies, waits for them, and re-layouts: 1.45 us -> 0 us
  Pallas kernels: 23.5 us -> 23.1 us
    unnamed x2 -> x0, local copies, waits for them, and re-layouts: 1.45 us -> none
    pallas_call x1, Pallas kernels: 23.5 us -> 22.2 us  [kernel_shards(): pl.pallas_call(functools.partial(kernel, deep), out_shape=(pltpu.VMEM((to...]
    pallas_call x0 -> x1, Pallas kernels: none -> 0.85 us  [kernel_shards(): pl.pallas_call(write_out, out_shape=(jax.ShapeDtypeStruct((tokens, width)...]
where the time goes in v2:
time: 23.8 us; the launch traced here: 23.7 us
  Pallas kernels  23.1 us (97%)
  between operations  0.64 us (3%)
    pallas_call x1, Pallas kernels, kernel_shards(): pl.pallas_call(functools.partial(kernel, deep), out_shape=(pltpu.VMEM((to...  22.2 us
    pallas_call x1, Pallas kernels, kernel_shards(): pl.pallas_call(write_out, out_shape=(jax.ShapeDtypeStruct((tokens, width)...  0.85 us

profile of v2, /device:TPU:0, one launch (start us, length us, event | category | flops | bytes accessed | tf_op | source)
XLA Modules:
  0.0 23.7 jit_solution(3441910626701938461)
XLA Ops:
  0.6 22.2 %shard_map.68 = (bf16[128,2048]{1,0:T(8,128)(2,1)S(1)}, f32[64,512]{1,0:T(8,128)S(1)}) custom-call(s32[16]{0:T(128)} %mask_hbm.1, s32[16]{0:T(128)} %list_hbm.1, bf16[128,2048]{1,0:T(8,128)(2,1)} %x_hbm.1, bf16[128,512]{1,0:T(8,128)(2,1)} %s_hbm.1, bf16[1024,512]{1,0:T(8,128)(2,1)} %w_hbm.1), custom_call_target="tpu_custom_call" | custom-call | tf_op jit(solution)/shard_map/pallas_call | solution.py:324
  22.8 0.8 %shard_map.69 = (bf16[128,2048]{1,0:T(8,128)(2,1)}, f32[64,512]{1,0:T(8,128)}) custom-call(bf16[128,2048]{1,0:T(8,128)(2,1)S(1)} %get-tuple-element.4.ig_ref, f32[64,512]{1,0:T(8,128)S(1)} %get-tuple-element.5.wg_ref), custom_call_target="tpu_custom_call" | custom-call | tf_op jit(solution)/shard_map/pallas_call | solution.py:357

commit v3 on v2

--- a/solution.py
+++ b/solution.py
@@ -11,7 +11,8 @@
 CORES = 2
 WIDE = 2
 HALVES = 2
-LAG = 2
+LAG = 4
+ORDERS = {4: ((3, 1, 2), (0, 3, 2), (0, 3, 1), (0, 2, 1))}
 SMALL = 1 << 20
 STEPS = 32766.0
 TINY = 1e-33
@@ -170,11 +171,15 @@
 
     span = WIDE * CORES * 2 * rows
 
+    orders = ORDERS.get(deep) or [[p for p in range(deep) if p != own] for own in range(deep)]
+
     def plane(n):
         if n == deep - 1:
             return z
-        down = jnp.where(deep - 1 - n > z, deep - 1 - n, deep - 2 - n)
-        return jnp.where(z < deep // 2, down, jnp.where(n < z, n, n + 1))
+        there = jnp.int32(0)
+        for own in range(deep):
+            there = jnp.where(z == own, orders[own][n], there)
+        return there
 
     def turn(n):
         part = x_v[:, pl.ds(pl.multiple_of(plane(n) * span, span), span)].T

time: 23.8 us -> 22.7 us (0.954)
  Pallas kernels: 23.1 us -> 21.8 us
    pallas_call x1, Pallas kernels: 22.2 us -> 20.9 us  [kernel_shards(): pl.pallas_call(functools.partial(kernel, deep), out_shape=(pltpu.VMEM((to...]
where the time goes in v3:
time: 22.7 us; the launch traced here: 22.4 us
  Pallas kernels  21.8 us (96%)
  between operations  0.64 us (3%)
    pallas_call x1, Pallas kernels, kernel_shards(): pl.pallas_call(functools.partial(kernel, deep), out_shape=(pltpu.VMEM((to...  20.9 us
    pallas_call x1, Pallas kernels, kernel_shards(): pl.pallas_call(write_out, out_shape=(jax.ShapeDtypeStruct((tokens, width)...  0.85 us

profile of v3, /device:TPU:0, one launch (start us, length us, event | category | flops | bytes accessed | tf_op | source)
XLA Modules:
  0.0 22.4 jit_solution(13042322308510839334)
XLA Ops:
  0.6 20.9 %shard_map.68 = (bf16[128,2048]{1,0:T(8,128)(2,1)S(1)}, f32[64,512]{1,0:T(8,128)S(1)}) custom-call(s32[16]{0:T(128)} %mask_hbm.1, s32[16]{0:T(128)} %list_hbm.1, bf16[128,2048]{1,0:T(8,128)(2,1)} %x_hbm.1, bf16[128,512]{1,0:T(8,128)(2,1)} %s_hbm.1, bf16[1024,512]{1,0:T(8,128)(2,1)} %w_hbm.1), custom_call_target="tpu_custom_call" | custom-call | tf_op jit(solution)/shard_map/pallas_call | solution.py:329
  21.6 0.8 %shard_map.69 = (bf16[128,2048]{1,0:T(8,128)(2,1)}, f32[64,512]{1,0:T(8,128)}) custom-call(bf16[128,2048]{1,0:T(8,128)(2,1)S(1)} %get-tuple-element.4.ig_ref, f32[64,512]{1,0:T(8,128)S(1)} %get-tuple-element.5.wg_ref), custom_call_target="tpu_custom_call" | custom-call | tf_op jit(solution)/shard_map/pallas_call | solution.py:362

commit v4 on v3

--- a/solution.py
+++ b/solution.py
@@ -11,8 +11,9 @@
 CORES = 2
 WIDE = 2
 HALVES = 2
-LAG = 4
-ORDERS = {4: ((3, 1, 2), (0, 3, 2), (0, 3, 1), (0, 2, 1))}
+STRIPS = 4
+LAG = 1
+ORDERS = {4: ((3, 2, 1), (0, 3, 2), (0, 3, 1), (0, 1, 2))}
 SMALL = 1 << 20
 STEPS = 32766.0
 TINY = 1e-33
@@ -73,10 +74,11 @@
     mask_hbm, list_hbm, x_hbm, s_hbm, w_hbm,
     ig_ref, wg_ref,
     mask_ref, list_ref,
-    x_v, s_v, w_v, tx, rx, own_part, px_send, px_scale, px_recv, px_rscale,
-    q, q_send, q_scale, zr, zr_scale, ig_send,
+    x_v, s_v, w_v, lead_tx, lead_rx, tx, rx,
+    lead_part, lead_send, lead_scale, lead_recv, lead_rscale, lead_q, lead_qscale,
+    own_part, px_send, px_scale, px_recv, px_rscale, q, q_send, q_scale, zr, zr_scale, ig_send,
     load_sem, s_send_sem, s_recv_sem, x_send_sem, x_recv_sem,
-    px_send_sem, px_recv_sem, z_send_sem, z_recv_sem, ig_send_sem, ig_recv_sem, hello,
+    px_send_sem, lead_recv_sem, px_recv_sem, z_send_sem, z_recv_sem, ig_send_sem, ig_recv_sem, hello,
 ):
     grp = lax.axis_index("grp")
     y = lax.axis_index("fsdp")
@@ -90,7 +92,8 @@
     half = w_hbm.shape[0]
     part_tokens = tokens // 2
     part_rows = rows // HALVES
-    pieces = deep * HALVES
+    pieces = (deep - 1) * HALVES
+    strip = s_hbm.shape[1] // STRIPS
 
     def at(zz, xx, cc, yy):
         return ((zz * WIDE + xx) * CORES + cc, yy)
@@ -126,13 +129,16 @@
         pl.semaphore_signal(barrier, inc=1, device_id=above, device_id_type=MESH)
 
     load_x = pltpu.make_async_copy(x_hbm, x_v, load_sem.at[0])
-    load_s = pltpu.make_async_copy(s_hbm, s_v.at[me], load_sem.at[1])
     load_w = pltpu.make_async_copy(w_hbm, w_v, load_sem.at[2])
     load_mask = pltpu.make_async_copy(mask_hbm, mask_ref, load_sem.at[3])
     load_list = pltpu.make_async_copy(list_hbm, list_ref, load_sem.at[4])
-    loads = [load_x, load_s, load_w, load_mask, load_list]
-    for load in loads:
-        load.start()
+    columns = [pl.ds(k * strip, strip) for k in range(STRIPS)]
+    load_x.start()
+    for k in range(STRIPS):
+        pltpu.make_async_copy(s_hbm.at[:, columns[k]], s_v.at[k, me], load_sem.at[1]).start()
+    load_w.start()
+    load_mask.start()
+    load_list.start()
 
     first, second = pl.ds(0, part_tokens), pl.ds(part_tokens, part_tokens)
     def received(ref, sem):
@@ -141,13 +147,19 @@
     def sent(ref, sem):
         remote(ref, ref, sem, sem, sibling).wait_send()
 
-    s_y = remote(s_hbm.at[first], s_v.at[me, first], s_send_sem, s_recv_sem.at[0], y_peer)
-    s_cross = remote(s_hbm.at[second], s_v.at[me, second], s_send_sem, s_recv_sem.at[0], y_cross)
-    s_sib = remote(s_hbm, s_v.at[me], s_send_sem, s_recv_sem.at[1], sibling)
-    forward_y = remote(s_v.at[from_y, first], s_v.at[from_y, first], s_send_sem, s_recv_sem.at[1], sibling)
-    forward_cross = remote(
-        s_v.at[from_cross, second], s_v.at[from_cross, second], s_send_sem, s_recv_sem.at[1], sibling
-    )
+    def send_strip(k):
+        own = s_v.at[k, me]
+        remote(s_hbm.at[first, columns[k]], own.at[first], s_send_sem, s_recv_sem.at[k, 0], y_peer).start()
+        remote(s_hbm.at[second, columns[k]], own.at[second], s_send_sem, s_recv_sem.at[k, 0], y_cross).start()
+        remote(s_hbm.at[:, columns[k]], own, s_send_sem, s_recv_sem.at[k, 1], sibling).start()
+
+    def forward_strip(k):
+        received(s_v.at[k, me], s_recv_sem.at[k, 0])
+        for landed in (s_v.at[k, from_y, first], s_v.at[k, from_cross, second]):
+            remote(landed, landed, s_send_sem, s_recv_sem.at[k, 1], sibling).start()
+
+    def strip_here(k):
+        received(s_v.at[k, 0:2], s_recv_sem.at[k, 1])
 
     @pl.when(jnp.logical_and(z > 0, z < deep - 1))
     def _():
@@ -157,9 +169,7 @@
     def _():
         pl.semaphore_wait(barrier, len(partners) + 1)
 
-    s_y.start()
-    s_cross.start()
-    s_sib.start()
+    send_strip(0)
 
     @pl.when(z == deep - 2)
     def _():
@@ -185,16 +195,27 @@
         part = x_v[:, pl.ds(pl.multiple_of(plane(n) * span, span), span)].T
         for xx in range(WIDE):
             for cy in range(CORES * 2):
+                start = (xx * CORES * 2 + cy) * rows
+                if n == 0:
+                    lead_tx[cy, xx * rows:(xx + 1) * rows, :] = part[start:start + rows, :]
+                    continue
                 for h in range(HALVES):
-                    start = (xx * CORES * 2 + cy) * rows + h * part_rows
-                    tx[n * HALVES + h, cy, xx * part_rows:(xx + 1) * part_rows, :] = part[start:start + part_rows, :]
-
+                    top = start + h * part_rows
+                    tx[(n - 1) * HALVES + h, cy, xx * part_rows:(xx + 1) * part_rows, :] = part[top:top + part_rows, :]
+
+    there_of = ((y_peer, from_y), (y_cross, from_cross), (sibling, from_sib))
     load_x.wait()
-    for n in range(deep):
+    turn(0)
+    for device, there in there_of:
+        remote(lead_tx.at[there], lead_rx.at[me], x_send_sem.at[0], x_recv_sem.at[pieces], device).start()
+    for k in range(1, STRIPS):
+        send_strip(k)
+    lead_rx[me] = lead_tx[me]
+    for n in range(1, deep):
         turn(n)
-        for j in range(n * HALVES, (n + 1) * HALVES):
-            for device, there in ((y_peer, from_y), (y_cross, from_cross), (sibling, from_sib)):
-                remote(tx.at[j, there], rx.at[j, me], x_send_sem, x_recv_sem.at[j], device).start()
+        for j in range((n - 1) * HALVES, n * HALVES):
+            for device, there in there_of:
+                remote(tx.at[j, there], rx.at[j, me], x_send_sem.at[1], x_recv_sem.at[j], device).start()
             rx[j, me] = tx[j, me]
 
     load_mask.wait()
@@ -210,7 +231,7 @@
         total = jnp.full((1, wg_ref.shape[1]), tally, jnp.int32).astype(jnp.float32)
         scales.append(done / (total + 1.0 - done))
 
-    load_s.wait()
+    pltpu.make_async_copy(s_v.at[:, me], s_v.at[:, me], load_sem.at[1]).wait()
     load_w.wait()
 
     def grad(s_block):
@@ -218,80 +239,126 @@
             s_block, w_v[...], (((1,), (1,)), ((), ())), preferred_element_type=jnp.float32
         ).astype(jnp.bfloat16)
 
+    def joined(part):
+        return jnp.concatenate([part(k) for k in range(STRIPS)], axis=1)
+
     own_columns = pl.ds(pl.multiple_of(y * half, half), half)
-    ig_ref[:, own_columns] = grad(s_v[me])
-
-    received(s_v.at[me], s_recv_sem.at[0])
-    forward_y.start()
-    forward_cross.start()
-    ig_send[...] = grad(jnp.concatenate([s_v[from_y, first], s_v[from_cross, second]], axis=0))
-    remote(ig_send.at[first], ig_ref.at[first, own_columns], ig_send_sem, ig_recv_sem, y_peer).start()
-    remote(ig_send.at[second], ig_ref.at[second, own_columns], ig_send_sem, ig_recv_sem, y_cross).start()
-
-    @pl.when(jnp.logical_and(z > 0, z < deep - 2))
-    def _():
-        pl.semaphore_wait(hello.at[0], 1)
-        pl.semaphore_signal(hello.at[0], inc=1, device_id=below, device_id_type=MESH)
-
-    @pl.when(jnp.logical_and(z > 1, z < deep - 1))
-    def _():
-        pl.semaphore_wait(hello.at[1], 1)
-        pl.semaphore_signal(hello.at[1], inc=1, device_id=above, device_id_type=MESH)
-
-    received(s_v.at[0:2], s_recv_sem.at[1])
+    ig_ref[:, own_columns] = grad(joined(lambda k: s_v[k, me]))
+
+    def other_grad():
+        block = [joined(lambda k: s_v[k, from_y, first]), joined(lambda k: s_v[k, from_cross, second])]
+        ig_send[...] = grad(jnp.concatenate(block, axis=0))
+        for tokens_of, device in ((first, y_peer), (second, y_cross)):
+            remote(
+                ig_send.at[tokens_of], ig_ref.at[tokens_of, own_columns], ig_send_sem, ig_recv_sem, device
+            ).start()
+
+    def product(lefts, rights, width):
+        total = None
+        for cc in range(CORES):
+            left = jnp.concatenate([lefts(cc * 2), lefts(cc * 2 + 1)], axis=1)
+            term = scales[cc][:, :width] * jnp.dot(left, rights(cc), preferred_element_type=jnp.float32)
+            total = term if total is None else total + term
+        return total
+
+    def lead_partial(k):
+        total = product(
+            lambda cy: lead_rx[cy], lambda cc: s_v[k, cc * 2:cc * 2 + 2].reshape(2 * tokens, strip), strip
+        )
+        lead_part[k, 0] = total[:rows]
+        lead_part[k, 1] = total[rows:]
+        lead_send[k], lead_scale[k] = encode(lead_part[k, 1 - wide])
+        remote(lead_send.at[k], lead_recv.at[k], px_send_sem.at[0], lead_recv_sem.at[k, 0], x_peer).start()
+        remote(lead_scale.at[k], lead_rscale.at[k], px_send_sem.at[1], lead_recv_sem.at[k, 1], x_peer).start()
+
+    def lead_gather(k):
+        received(lead_recv.at[k], lead_recv_sem.at[k, 0])
+        received(lead_rscale.at[k], lead_recv_sem.at[k, 1])
+        coded, scale = encode(lead_part[k, wide] + decoded(lead_recv[k], lead_rscale[k]))
+        for h in range(HALVES):
+            lead_q[k, h] = coded[h * part_rows:(h + 1) * part_rows]
+            lead_qscale[k, h] = scale
+        there = at(plane(0), wide, core, y)
+        for slot, (src, dst) in enumerate(((lead_q, zr), (lead_qscale, zr_scale))):
+            remote(
+                src.at[k], dst.at[z, :, :, columns[k]], z_send_sem.at[slot], z_recv_sem.at[z, slot], there
+            ).start()
 
     def partial(j):
         received(rx.at[j, 0:3], x_recv_sem.at[j])
-        total = None
-        for cc in range(CORES):
-            left = jnp.concatenate([rx[j, cc * 2], rx[j, cc * 2 + 1]], axis=1)
-            right = s_v[cc * 2:cc * 2 + 2].reshape(2 * tokens, s_v.shape[2])
-            product = scales[cc] * jnp.dot(left, right, preferred_element_type=jnp.float32)
-            total = product if total is None else total + product
+        total = product(
+            lambda cy: rx[j, cy],
+            lambda cc: joined(lambda k: s_v[k, cc * 2:cc * 2 + 2].reshape(2 * tokens, strip)),
+            s_hbm.shape[1],
+        )
         own_part[j, 0] = total[:part_rows]
         own_part[j, 1] = total[part_rows:]
-        coded, scale = encode(own_part[j, 1 - wide])
-        px_send[j] = coded
-        px_scale[j] = scale
-        remote(px_send.at[j], px_recv.at[j], px_send_sem.at[0], px_recv_sem.at[j, 0], x_peer).start()
-        remote(px_scale.at[j], px_rscale.at[j], px_send_sem.at[1], px_recv_sem.at[j, 1], x_peer).start()
-
-    def gather_x(j):
-        n, h = j // HALVES, j % HALVES
-        if j == 0:
-            @pl.when(z == 0)
-            def _():
-                pl.semaphore_wait(hello.at[0], 1)
-
-            @pl.when(z == deep - 1)
-            def _():
-                pl.semaphore_wait(hello.at[1], 1)
-
+        px_send[j], px_scale[j] = encode(own_part[j, 1 - wide])
+        remote(px_send.at[j], px_recv.at[j], px_send_sem.at[2], px_recv_sem.at[j, 0], x_peer).start()
+        remote(px_scale.at[j], px_rscale.at[j], px_send_sem.at[3], px_recv_sem.at[j, 1], x_peer).start()
+
+    def gather(j):
+        n, h = 1 + j // HALVES, j % HALVES
         received(px_recv.at[j], px_recv_sem.at[j, 0])
         received(px_rscale.at[j], px_recv_sem.at[j, 1])
         value = own_part[j, wide] + decoded(px_recv[j], px_rscale[j])
-        if n < deep - 1:
-            coded, scale = encode(value)
-            q_send[j] = coded
-            q_scale[j] = scale
-            there = at(plane(n), wide, core, y)
-            remote(q_send.at[j], zr.at[z, h], z_send_sem.at[0], z_recv_sem.at[z, 0], there).start()
-            remote(q_scale.at[j], zr_scale.at[z, h], z_send_sem.at[1], z_recv_sem.at[z, 1], there).start()
-        else:
+        if n == deep - 1:
             q[h] = value
-
-    for j in range(pieces + LAG):
-        if j < pieces:
-            partial(j)
+            return
+        q_send[j], q_scale[j] = encode(value)
+        there = at(plane(n), wide, core, y)
+        remote(q_send.at[j], zr.at[z, h], z_send_sem.at[2], z_recv_sem.at[z, 0], there).start()
+        remote(q_scale.at[j], zr_scale.at[z, h], z_send_sem.at[3], z_recv_sem.at[z, 1], there).start()
+
+    @pl.when(jnp.logical_and(z > 0, z < deep - 2))
+    def _():
+        pl.semaphore_wait(hello.at[0], 1)
+        pl.semaphore_signal(hello.at[0], inc=1, device_id=below, device_id_type=MESH)
+
+    @pl.when(jnp.logical_and(z > 1, z < deep - 1))
+    def _():
+        pl.semaphore_wait(hello.at[1], 1)
+        pl.semaphore_signal(hello.at[1], inc=1, device_id=above, device_id_type=MESH)
+
+    forward_strip(0)
+    strip_here(0)
+    received(lead_rx.at[0:3], x_recv_sem.at[pieces])
+    lead_partial(0)
+    forward_strip(1)
+    for k in range(1, STRIPS - 1):
+        forward_strip(k + 1)
+        strip_here(k)
+        lead_partial(k)
+
+    @pl.when(z == 0)
+    def _():
+        pl.semaphore_wait(hello.at[0], 1)
+
+    @pl.when(z == deep - 1)
+    def _():
+        pl.semaphore_wait(hello.at[1], 1)
+
+    lead_gather(0)
+    strip_here(STRIPS - 1)
+    lead_partial(STRIPS - 1)
+    other_grad()
+
+    steps = [functools.partial(lead_gather, k) for k in range(1, STRIPS)]
+    steps += [functools.partial(gather, j) for j in range(pieces)]
+    for j in range(pieces):
+        partial(j)
         if j >= LAG:
-            gather_x(j - LAG)
-
-    sent(s_v.at[0:3], s_send_sem)
-    sent(tx.at[:, 0:3], x_send_sem)
-    sent(px_send, px_send_sem.at[0])
-    sent(px_scale, px_send_sem.at[1])
-    sent(q_send, z_send_sem.at[0])
-    sent(q_scale, z_send_sem.at[1])
+            steps.pop(0)()
+    for step in steps:
+        step()
+
+    sent(s_v.at[:, 0:3], s_send_sem)
+    sent(lead_tx.at[0:3], x_send_sem.at[0])
+    sent(tx.at[:, 0:3], x_send_sem.at[1])
+    for slot, ref in enumerate((lead_send, lead_scale, px_send, px_scale)):
+        sent(ref, px_send_sem.at[slot])
+    for slot, ref in enumerate((lead_q, lead_qscale, q_send, q_scale)):
+        sent(ref, z_send_sem.at[slot])
     sent(ig_send, ig_send_sem)
 
     for n in range(deep - 1):
@@ -325,7 +392,7 @@
     f32, bf16, i16 = jnp.float32, jnp.bfloat16, jnp.int16
     dma = pltpu.SemaphoreType.DMA
     anywhere = pl.BlockSpec(memory_space=pl.ANY)
-    part_rows, pieces = rows // HALVES, deep * HALVES
+    part_rows, pieces, strip = rows // HALVES, (deep - 1) * HALVES, values // STRIPS
     on_chip = pl.pallas_call(
         functools.partial(kernel, deep),
         out_shape=(
@@ -338,10 +405,19 @@
             pltpu.SMEM(mask.shape, jnp.int32),
             pltpu.SMEM(plist.shape, jnp.int32),
             pltpu.VMEM((tokens, width), bf16),
-            pltpu.VMEM((CORES * 2, tokens, values), bf16),
+            pltpu.VMEM((STRIPS, CORES * 2, tokens, strip), bf16),
             pltpu.VMEM(w.shape, bf16),
+            pltpu.VMEM((CORES * 2, WIDE * rows, tokens), bf16),
+            pltpu.VMEM((CORES * 2, WIDE * rows, tokens), bf16),
             pltpu.VMEM((pieces, CORES * 2, WIDE * part_rows, tokens), bf16),
             pltpu.VMEM((pieces, CORES * 2, WIDE * part_rows, tokens), bf16),
+            pltpu.VMEM((STRIPS, WIDE, rows, strip), f32),
+            pltpu.VMEM((STRIPS, rows, strip), i16),
+            pltpu.VMEM((STRIPS, 1, strip), f32),
+            pltpu.VMEM((STRIPS, rows, strip), i16),
+            pltpu.VMEM((STRIPS, 1, strip), f32),
+            pltpu.VMEM((STRIPS, HALVES, part_rows, strip), i16),
+            pltpu.VMEM((STRIPS, HALVES, 1, strip), f32),
             pltpu.VMEM((pieces, WIDE, part_rows, values), f32),
             pltpu.VMEM((pieces, part_rows, values), i16),
             pltpu.VMEM((pieces, 1, values), f32),
@@ -353,8 +429,8 @@
             pltpu.VMEM((deep, HALVES, part_rows, values), i16),
             pltpu.VMEM((deep, HALVES, 1, values), f32),
             pltpu.VMEM((tokens, w.shape[0]), bf16),
-            dma((5,)), dma, dma((2,)), dma, dma((pieces,)),
-            dma((2,)), dma((pieces, 2)), dma((2,)), dma((deep, 2)), dma, dma,
+            dma((5,)), dma, dma((STRIPS, 2)), dma((2,)), dma((pieces + 1,)),
+            dma((4,)), dma((STRIPS, 2)), dma((pieces, 2)), dma((4,)), dma((deep, 2)), dma, dma,
             pltpu.SemaphoreType.REGULAR((2,)),
         ],
         compiler_params=pltpu.CompilerParams(collective_id=0, has_side_effects=True),
@@ -377,7 +453,7 @@
 
     def shards(x, s, w, mask, plist):
         rows = x.shape[1] // (outer * inner)
-        if inner == 2 and outer % (CORES * WIDE) == 0 and outer // (CORES * WIDE) >= 4 and rows % (16 * HALVES) == 0 and x.shape[0] % 128 == 0:
+        if inner == 2 and outer % (CORES * WIDE) == 0 and outer // (CORES * WIDE) >= 4 and rows % (16 * HALVES) == 0 and x.shape[0] % 128 == 0 and s.shape[1] % (128 * STRIPS) == 0:
             return tuple(kernel_shards(outer // (CORES * WIDE), rows, x, s, w, mask, plist))
         return collective_shards(x, s, w, mask, plist)
 

time: 22.7 us -> 22.5 us (level)
  the two profiles are of different devices: /device:TPU:0 before, /device:TPU:8 now
where the time goes in v4:
time: 22.5 us; the launch traced here: 22.3 us
  Pallas kernels  21.7 us (96%)
  between operations  0.64 us (3%)
    pallas_call x1, Pallas kernels, kernel_shards(): pl.pallas_call(functools.partial(kernel, deep), out_shape=(pltpu.VMEM((to...  20.8 us
    pallas_call x1, Pallas kernels, kernel_shards(): pl.pallas_call(write_out, out_shape=(jax.ShapeDtypeStruct((tokens, width)...  0.85 us

profile of v4, /device:TPU:8, one launch (start us, length us, event | category | flops | bytes accessed | tf_op | source)
XLA Modules:
  0.0 22.3 jit_solution(12765720726708474389)
XLA Ops:
  0.6 20.8 %shard_map.68 = (bf16[128,2048]{1,0:T(8,128)(2,1)S(1)}, f32[64,512]{1,0:T(8,128)S(1)}) custom-call(s32[16]{0:T(128)} %mask_hbm.1, s32[16]{0:T(128)} %list_hbm.1, bf16[128,2048]{1,0:T(8,128)(2,1)} %x_hbm.1, bf16[128,512]{1,0:T(8,128)(2,1)} %s_hbm.1, bf16[1024,512]{1,0:T(8,128)(2,1)} %w_hbm.1), custom_call_target="tpu_custom_call" | custom-call | tf_op jit(solution)/shard_map/pallas_call | solution.py:396
  21.5 0.8 %shard_map.69 = (bf16[128,2048]{1,0:T(8,128)(2,1)}, f32[64,512]{1,0:T(8,128)}) custom-call(bf16[128,2048]{1,0:T(8,128)(2,1)S(1)} %get-tuple-element.4.ig_ref, f32[64,512]{1,0:T(8,128)S(1)} %get-tuple-element.5.wg_ref), custom_call_target="tpu_custom_call" | custom-call | tf_op jit(solution)/shard_map/pallas_call | solution.py:438

commit v5 on v4

--- a/solution.py
+++ b/solution.py
@@ -13,6 +13,7 @@
 HALVES = 2
 STRIPS = 4
 LAG = 1
+GRAD_AFTER = 1
 ORDERS = {4: ((3, 2, 1), (0, 3, 2), (0, 3, 1), (0, 1, 2))}
 SMALL = 1 << 20
 STEPS = 32766.0
@@ -268,8 +269,8 @@
         lead_part[k, 0] = total[:rows]
         lead_part[k, 1] = total[rows:]
         lead_send[k], lead_scale[k] = encode(lead_part[k, 1 - wide])
+        remote(lead_scale.at[k], lead_rscale.at[k], px_send_sem.at[1], lead_recv_sem.at[k, 1], x_peer).start()
         remote(lead_send.at[k], lead_recv.at[k], px_send_sem.at[0], lead_recv_sem.at[k, 0], x_peer).start()
-        remote(lead_scale.at[k], lead_rscale.at[k], px_send_sem.at[1], lead_recv_sem.at[k, 1], x_peer).start()
 
     def lead_gather(k):
         received(lead_recv.at[k], lead_recv_sem.at[k, 0])
@@ -279,7 +280,7 @@
             lead_q[k, h] = coded[h * part_rows:(h + 1) * part_rows]
             lead_qscale[k, h] = scale
         there = at(plane(0), wide, core, y)
-        for slot, (src, dst) in enumerate(((lead_q, zr), (lead_qscale, zr_scale))):
+        for slot, (src, dst) in ((1, (lead_qscale, zr_scale)), (0, (lead_q, zr))):
             remote(
                 src.at[k], dst.at[z, :, :, columns[k]], z_send_sem.at[slot], z_recv_sem.at[z, slot], there
             ).start()
@@ -294,8 +295,8 @@
         own_part[j, 0] = total[:part_rows]
         own_part[j, 1] = total[part_rows:]
         px_send[j], px_scale[j] = encode(own_part[j, 1 - wide])
+        remote(px_scale.at[j], px_rscale.at[j], px_send_sem.at[3], px_recv_sem.at[j, 1], x_peer).start()
         remote(px_send.at[j], px_recv.at[j], px_send_sem.at[2], px_recv_sem.at[j, 0], x_peer).start()
-        remote(px_scale.at[j], px_rscale.at[j], px_send_sem.at[3], px_recv_sem.at[j, 1], x_peer).start()
 
     def gather(j):
         n, h = 1 + j // HALVES, j % HALVES
@@ -307,8 +308,8 @@
             return
         q_send[j], q_scale[j] = encode(value)
         there = at(plane(n), wide, core, y)
+        remote(q_scale.at[j], zr_scale.at[z, h], z_send_sem.at[3], z_recv_sem.at[z, 1], there).start()
         remote(q_send.at[j], zr.at[z, h], z_send_sem.at[2], z_recv_sem.at[z, 0], there).start()
-        remote(q_scale.at[j], zr_scale.at[z, h], z_send_sem.at[3], z_recv_sem.at[z, 1], there).start()
 
     @pl.when(jnp.logical_and(z > 0, z < deep - 2))
     def _():
@@ -341,12 +342,13 @@
     lead_gather(0)
     strip_here(STRIPS - 1)
     lead_partial(STRIPS - 1)
-    other_grad()
 
     steps = [functools.partial(lead_gather, k) for k in range(1, STRIPS)]
     steps += [functools.partial(gather, j) for j in range(pieces)]
     for j in range(pieces):
         partial(j)
+        if j == GRAD_AFTER:
+            other_grad()
         if j >= LAG:
             steps.pop(0)()
     for step in steps:
@@ -357,9 +359,6 @@
     sent(tx.at[:, 0:3], x_send_sem.at[1])
     for slot, ref in enumerate((lead_send, lead_scale, px_send, px_scale)):
         sent(ref, px_send_sem.at[slot])
-    for slot, ref in enumerate((lead_q, lead_qscale, q_send, q_scale)):
-        sent(ref, z_send_sem.at[slot])
-    sent(ig_send, ig_send_sem)
 
     for n in range(deep - 1):
         source = jnp.where(n < z, n, n + 1)
@@ -373,6 +372,9 @@
                 wg_ref[h * part_rows:(h + 1) * part_rows, :] = q[h] + value
 
     received(ig_send, ig_recv_sem)
+    for slot, ref in enumerate((lead_q, lead_qscale, q_send, q_scale)):
+        sent(ref, z_send_sem.at[slot])
+    sent(ig_send, ig_send_sem)
 
 
 def write_out(ig_ref, wg_ref, ig_hbm, wg_hbm, sems):

time: 22.5 us -> 22.2 us (0.987)
  the two profiles are of different devices: /device:TPU:8 before, /device:TPU:0 now
where the time goes in v5:
time: 22.2 us; the launch traced here: 22 us
  Pallas kernels  21.4 us (96%)
  between operations  0.64 us (3%)
    pallas_call x1, Pallas kernels, kernel_shards(): pl.pallas_call(functools.partial(kernel, deep), out_shape=(pltpu.VMEM((to...  20.6 us
    pallas_call x1, Pallas kernels, kernel_shards(): pl.pallas_call(write_out, out_shape=(jax.ShapeDtypeStruct((tokens, width)...  0.85 us

profile of v5, /device:TPU:0, one launch (start us, length us, event | category | flops | bytes accessed | tf_op | source)
XLA Modules:
  0.0 22.0 jit_solution(13531123051163742801)
XLA Ops:
  0.6 20.6 %shard_map.68 = (bf16[128,2048]{1,0:T(8,128)(2,1)S(1)}, f32[64,512]{1,0:T(8,128)S(1)}) custom-call(s32[16]{0:T(128)} %mask_hbm.1, s32[16]{0:T(128)} %list_hbm.1, bf16[128,2048]{1,0:T(8,128)(2,1)} %x_hbm.1, bf16[128,512]{1,0:T(8,128)(2,1)} %s_hbm.1, bf16[1024,512]{1,0:T(8,128)(2,1)} %w_hbm.1), custom_call_target="tpu_custom_call" | custom-call | tf_op jit(solution)/shard_map/pallas_call | solution.py:398
  21.2 0.8 %shard_map.69 = (bf16[128,2048]{1,0:T(8,128)(2,1)}, f32[64,512]{1,0:T(8,128)}) custom-call(bf16[128,2048]{1,0:T(8,128)(2,1)S(1)} %get-tuple-element.4.ig_ref, f32[64,512]{1,0:T(8,128)S(1)} %get-tuple-element.5.wg_ref), custom_call_target="tpu_custom_call" | custom-call | tf_op jit(solution)/shard_map/pallas_call | solution.py:440

commit v6 on v5

--- a/solution.py
+++ b/solution.py
@@ -15,7 +15,7 @@
 LAG = 1
 GRAD_AFTER = 1
 ORDERS = {4: ((3, 2, 1), (0, 3, 2), (0, 3, 1), (0, 1, 2))}
-SMALL = 1 << 20
+SMALL = 1 << 21
 STEPS = 32766.0
 TINY = 1e-33
 
@@ -73,11 +73,11 @@
 def kernel(
     deep,
     mask_hbm, list_hbm, x_hbm, s_hbm, w_hbm,
-    ig_ref, wg_ref,
+    ig_ref, q, zr, zr_scale,
     mask_ref, list_ref,
     x_v, s_v, w_v, lead_tx, lead_rx, tx, rx,
     lead_part, lead_send, lead_scale, lead_recv, lead_rscale, lead_q, lead_qscale,
-    own_part, px_send, px_scale, px_recv, px_rscale, q, q_send, q_scale, zr, zr_scale, ig_send,
+    own_part, px_send, px_scale, px_recv, px_rscale, q_send, q_scale, ig_send,
     load_sem, s_send_sem, s_recv_sem, x_send_sem, x_recv_sem,
     px_send_sem, lead_recv_sem, px_recv_sem, z_send_sem, z_recv_sem, ig_send_sem, ig_recv_sem, hello,
 ):
@@ -89,7 +89,7 @@
     oy, oc = 1 - y, 1 - core
     tokens = s_hbm.shape[0]
     groups = mask_ref.shape[0]
-    rows = wg_ref.shape[0]
+    rows = q.shape[0] * q.shape[1]
     half = w_hbm.shape[0]
     part_tokens = tokens // 2
     part_rows = rows // HALVES
@@ -228,8 +228,8 @@
         tally = jnp.int32(0)
         for h in range(groups):
             tally = tally + jnp.where(list_ref[h] == mine, mask_ref[h], 0)
-        done = jnp.full((1, wg_ref.shape[1]), mask_ref[here], jnp.int32).astype(jnp.float32)
-        total = jnp.full((1, wg_ref.shape[1]), tally, jnp.int32).astype(jnp.float32)
+        done = jnp.full((1, s_hbm.shape[1]), mask_ref[here], jnp.int32).astype(jnp.float32)
+        total = jnp.full((1, s_hbm.shape[1]), tally, jnp.int32).astype(jnp.float32)
         scales.append(done / (total + 1.0 - done))
 
     pltpu.make_async_copy(s_v.at[:, me], s_v.at[:, me], load_sem.at[1]).wait()
@@ -242,6 +242,9 @@
 
     def joined(part):
         return jnp.concatenate([part(k) for k in range(STRIPS)], axis=1)
+
+    zr[z] = jnp.zeros(zr.shape[1:], zr.dtype)
+    zr_scale[z] = jnp.zeros(zr_scale.shape[1:], zr_scale.dtype)
 
     own_columns = pl.ds(pl.multiple_of(y * half, half), half)
     ig_ref[:, own_columns] = grad(joined(lambda k: s_v[k, me]))
@@ -364,12 +367,6 @@
         source = jnp.where(n < z, n, n + 1)
         received(zr.at[source], z_recv_sem.at[source, 0])
         received(zr_scale.at[source], z_recv_sem.at[source, 1])
-        for h in range(HALVES):
-            value = decoded(zr[source, h], zr_scale[source, h])
-            if n < deep - 2:
-                q[h] = q[h] + value
-            else:
-                wg_ref[h * part_rows:(h + 1) * part_rows, :] = q[h] + value
 
     received(ig_send, ig_recv_sem)
     for slot, ref in enumerate((lead_q, lead_qscale, q_send, q_scale)):
@@ -377,15 +374,19 @@
     sent(ig_send, ig_send_sem)
 
 
-def write_out(ig_ref, wg_ref, ig_hbm, wg_hbm, sems):
-    copies = [
-        pltpu.make_async_copy(ig_ref, ig_hbm, sems.at[0]),
-        pltpu.make_async_copy(wg_ref, wg_hbm, sems.at[1]),
-    ]
-    for copy in copies:
-        copy.start()
-    for copy in copies:
-        copy.wait()
+def write_out(ig_ref, q, zr, zr_scale, ig_hbm, wg_hbm, wg_ref, sems):
+    ig_copy = pltpu.make_async_copy(ig_ref, ig_hbm, sems.at[0])
+    wg_copy = pltpu.make_async_copy(wg_ref, wg_hbm, sems.at[1])
+    ig_copy.start()
+    part_rows = q.shape[1]
+    for h in range(q.shape[0]):
+        total = q[h]
+        for source in range(zr.shape[0]):
+            total = total + decoded(zr[source, h], zr_scale[source, h])
+        wg_ref[h * part_rows:(h + 1) * part_rows, :] = total
+    wg_copy.start()
+    ig_copy.wait()
+    wg_copy.wait()
 
 
 def kernel_shards(deep, rows, x, s, w, mask, plist):
@@ -399,10 +400,12 @@
         functools.partial(kernel, deep),
         out_shape=(
             pltpu.VMEM((tokens, width), bf16),
-            pltpu.VMEM((rows, values), f32),
+            pltpu.VMEM((HALVES, part_rows, values), f32),
+            pltpu.VMEM((deep, HALVES, part_rows, values), i16),
+            pltpu.VMEM((deep, HALVES, 1, values), f32),
         ),
         in_specs=[anywhere] * 5,
-        out_specs=(pl.BlockSpec(memory_space=pltpu.VMEM),) * 2,
+        out_specs=(pl.BlockSpec(memory_space=pltpu.VMEM),) * 4,
         scratch_shapes=[
             pltpu.SMEM(mask.shape, jnp.int32),
             pltpu.SMEM(plist.shape, jnp.int32),
@@ -425,11 +428,8 @@
             pltpu.VMEM((pieces, 1, values), f32),
             pltpu.VMEM((pieces, part_rows, values), i16),
             pltpu.VMEM((pieces, 1, values), f32),
-            pltpu.VMEM((HALVES, part_rows, values), f32),
             pltpu.VMEM((pieces - HALVES, part_rows, values), i16),
             pltpu.VMEM((pieces - HALVES, 1, values), f32),
-            pltpu.VMEM((deep, HALVES, part_rows, values), i16),
-            pltpu.VMEM((deep, HALVES, 1, values), f32),
             pltpu.VMEM((tokens, w.shape[0]), bf16),
             dma((5,)), dma, dma((STRIPS, 2)), dma((2,)), dma((pieces + 1,)),
             dma((4,)), dma((STRIPS, 2)), dma((pieces, 2)), dma((4,)), dma((deep, 2)), dma, dma,
@@ -443,9 +443,9 @@
             jax.ShapeDtypeStruct((tokens, width), bf16),
             jax.ShapeDtypeStruct((rows, values), f32),
         ),
-        in_specs=[pl.BlockSpec(memory_space=pltpu.VMEM)] * 2,
+        in_specs=[pl.BlockSpec(memory_space=pltpu.VMEM)] * 4,
         out_specs=(anywhere,) * 2,
-        scratch_shapes=[dma((2,))],
+        scratch_shapes=[pltpu.VMEM((rows, values), f32), dma((2,))],
         compiler_params=pltpu.CompilerParams(vmem_limit_bytes=SMALL),
     )(*(pltpu.with_memory_space_constraint(part, pltpu.VMEM) for part in on_chip))
 

time: 22.2 us -> 22.2 us (level)
  no operation moved by 1% of the time
where the time goes in v6:
time: 22.2 us; the launch traced here: 22 us
  Pallas kernels  21.4 us (96%)
  between operations  0.64 us (3%)
    pallas_call x1, Pallas kernels, kernel_shards(): pl.pallas_call(functools.partial(kernel, deep), out_shape=(pltpu.VMEM((to...  20.5 us
    pallas_call x1, Pallas kernels, kernel_shards(): pl.pallas_call(write_out, out_shape=(jax.ShapeDtypeStruct((tokens, width)...  0.85 us

profile of v6, /device:TPU:0, one launch (start us, length us, event | category | flops | bytes accessed | tf_op | source)
XLA Modules:
  0.0 22.0 jit_solution(11756863034551654893)
XLA Ops:
  0.6 20.5 %shard_map.68 = (bf16[128,2048]{1,0:T(8,128)(2,1)S(1)}, f32[2,32,512]{2,1,0:T(8,128)S(1)}, s16[4,2,32,512]{3,2,1,0:T(8,128)(2,1)S(1)}, f32[4,2,1,512]{3,2,1,0:T(1,128)S(1)}) custom-call(s32[16]{0:T(128)} %mask_hbm.1, s32[16]{0:T(128)} %list_hbm.1, bf16[128,2048]{1,0:T(8,128)(2,1)} %x_hbm.1, bf16[128,512]{1,0:T(8,128)(2,1)} %s_hbm.1, bf16[1024,512]{1,0:T(8,128)(2,1)} %w_hbm.1), custom_call_target="tpu_custom_call" | custom-call | tf_op jit(solution)/shard_map/pallas_call | solution.py:399
  21.2 0.8 %shard_map.69 = (bf16[128,2048]{1,0:T(8,128)(2,1)}, f32[64,512]{1,0:T(8,128)}) custom-call(bf16[128,2048]{1,0:T(8,128)(2,1)S(1)} %get-tuple-element.6.ig_ref, f32[2,32,512]{2,1,0:T(8,128)S(1)} %get-tuple-element.7.q, s16[4,2,32,512]{3,2,1,0:T(8,128)(2,1)S(1)} %get-tuple-element.8.zr, f32[4,2,1,512]{3,2,1,0:T(1,128)S(1)} %get-tuple-element.9.zr_scale), custom_call_target="tpu_custom_call" | custom-call | tf_op jit(solution)/shard_map/pallas_call | solution.py:440

commit v7 on v6

--- a/solution.py
+++ b/solution.py
@@ -16,6 +16,7 @@
 GRAD_AFTER = 1
 ORDERS = {4: ((3, 2, 1), (0, 3, 2), (0, 3, 1), (0, 1, 2))}
 SMALL = 1 << 21
+SHARES = 4
 STEPS = 32766.0
 TINY = 1e-33
 
@@ -377,7 +378,10 @@
 def write_out(ig_ref, q, zr, zr_scale, ig_hbm, wg_hbm, wg_ref, sems):
     ig_copy = pltpu.make_async_copy(ig_ref, ig_hbm, sems.at[0])
     wg_copy = pltpu.make_async_copy(wg_ref, wg_hbm, sems.at[1])
-    ig_copy.start()
+    share = ig_ref.shape[0] // SHARES
+    for k in range(SHARES):
+        rows_of = pl.ds(k * share, share)
+        pltpu.make_async_copy(ig_ref.at[rows_of], ig_hbm.at[rows_of], sems.at[0]).start()
     part_rows = q.shape[1]
     for h in range(q.shape[0]):
         total = q[h]

time: 22.2 us -> 22.2 us (level)
  no operation moved by 1% of the time
where the time goes in v7:
time: 22.2 us; the launch traced here: 22 us
  Pallas kernels  21.4 us (96%)
  between operations  0.64 us (3%)
    pallas_call x1, Pallas kernels, kernel_shards(): pl.pallas_call(functools.partial(kernel, deep), out_shape=(pltpu.VMEM((to...  20.5 us
    pallas_call x1, Pallas kernels, kernel_shards(): pl.pallas_call(write_out, out_shape=(jax.ShapeDtypeStruct((tokens, width)...  0.85 us

profile of v7, /device:TPU:0, one launch (start us, length us, event | category | flops | bytes accessed | tf_op | source)
XLA Modules:
  0.0 22.0 jit_solution(4173250534386942556)
XLA Ops:
  0.6 20.5 %shard_map.68 = (bf16[128,2048]{1,0:T(8,128)(2,1)S(1)}, f32[2,32,512]{2,1,0:T(8,128)S(1)}, s16[4,2,32,512]{3,2,1,0:T(8,128)(2,1)S(1)}, f32[4,2,1,512]{3,2,1,0:T(1,128)S(1)}) custom-call(s32[16]{0:T(128)} %mask_hbm.1, s32[16]{0:T(128)} %list_hbm.1, bf16[128,2048]{1,0:T(8,128)(2,1)} %x_hbm.1, bf16[128,512]{1,0:T(8,128)(2,1)} %s_hbm.1, bf16[1024,512]{1,0:T(8,128)(2,1)} %w_hbm.1), custom_call_target="tpu_custom_call" | custom-call | tf_op jit(solution)/shard_map/pallas_call | solution.py:403
  21.2 0.8 %shard_map.69 = (bf16[128,2048]{1,0:T(8,128)(2,1)}, f32[64,512]{1,0:T(8,128)}) custom-call(bf16[128,2048]{1,0:T(8,128)(2,1)S(1)} %get-tuple-element.6.ig_ref, f32[2,32,512]{2,1,0:T(8,128)S(1)} %get-tuple-element.7.q, s16[4,2,32,512]{3,2,1,0:T(8,128)(2,1)S(1)} %get-tuple-element.8.zr, f32[4,2,1,512]{3,2,1,0:T(1,128)S(1)} %get-tuple-element.9.zr_scale), custom_call_target="tpu_custom_call" | custom-call | tf_op jit(solution)/shard_map/pallas_call | solution.py:444
